TPU v7x, 32 devices: a whole 2x2x4 slice. The times are simulated.
32 devices in a mesh: groups: 2 (over y), seq: 4 (over z), tp: 4 (over x, core).
Axes of the slice: x: 2, y: 2, z: 4, core: 2. Of those that a mesh axis runs over, the one named last changes fastest.
Arguments:
- prompt_kv: bfloat16 [32768, 64, 128], P(('groups', 'seq', 'tp')), parts along dimension 0, may hold values from -6 to 6
- prompt_length: int32 [2], P('groups'), parts along dimension 0, may hold values from 8192 to 16384
- queries: bfloat16 [16, 4096], P('groups'), parts along dimension 0, may hold values from -6 to 6
- new_kv: bfloat16 [16, 16, 2, 128], P('groups'), parts along dimension 0, may hold values from -6 to 6
- k_cache: bfloat16 [256, 8192, 128], P(('groups', 'seq'), 'tp'), parts along dimension 0, may hold values from -6 to 6
- v_cache: bfloat16 [256, 8192, 128], P(('groups', 'seq'), 'tp'), parts along dimension 0, may hold values from -6 to 6
- lengths: int32 [16], P('groups'), parts along dimension 0, may hold values from 4097 to 8192
- slots: int32 [16], P('groups'), parts along dimension 0, may hold values from 0 to 7, each once
Outputs:
- prompt_owned: bfloat16 [32768, 64, 128], P(('groups', 'tp'), 'seq'), parts along dimension 0
- attended: bfloat16 [256, 256], P(('groups', 'seq')), parts along dimension 0
There are 2 independent parts, one for each index of `groups`. A program takes and returns all parts, laid end to end along the dimension named above; each array names one. Nothing has to cross between parts.
Inputs may be any that keep to these rules, and one draw needn't show every extreme that they name: `slots`: each slot once.
All inputs are finite; a program needn't handle non-finite values.
Results may differ from a plain program's by a relative error of at most 0.0028.
Values may be sent and summed in bfloat16 or wider, within the bound.
No kernel may reach another device: no remote copies, remote signals or barrier semaphores. Data moves between devices by JAX's collectives and lax.ppermute only.
A program may use at most 128 MiB of HBM per device.

v0:
```python
import jax
import jax.numpy as jnp
from jax import lax
from jax.sharding import PartitionSpec as P

query_scale = 168.0 ** (-0.5)
negative = -1e30


def merged(part, axis, combine):
    gathered = jax.tree.map(lambda a: lax.all_gather(a, axis), part)

    def take(source):
        return jax.tree.map(lambda a: lax.dynamic_index_in_dim(a, source, 0, False), gathered)

    return lax.fori_loop(
        1, lax.axis_size(axis), lambda source, state: combine(state, take(source)), take(0)
    )


def combine_parts(first, second):
    upper = jnp.maximum(first[0], second[0])
    scale_one = jnp.exp(first[0] - upper)
    scale_two = jnp.exp(second[0] - upper)
    total = first[1] * scale_one + second[1] * scale_two
    summed = first[2] * scale_one[..., None] + second[2] * scale_two[..., None]
    return (upper, total, summed)


def per_device(prompt_kv, prompt_length, queries, new_kv, k_cache, v_cache, lengths, slots):
    block = prompt_kv.shape[0]
    offset = (lax.axis_index("seq") * lax.axis_size("tp") + lax.axis_index("tp")) * block
    position = offset + jnp.arange(block, dtype=jnp.int32)
    kept = jnp.where(
        (position < prompt_length[0])[:, None, None], prompt_kv, jnp.zeros_like(prompt_kv)
    )
    prompt_owned = lax.all_to_all(kept, "seq", split_axis=1, concat_axis=0, tiled=True)
    resident = lengths.shape[0]
    pair_rows = k_cache.shape[0]
    span = k_cache.shape[1]
    width = k_cache.shape[2]
    heads = new_kv.shape[1]
    group = queries.shape[1] // (heads * width)
    rows = lax.axis_index("seq") * pair_rows + jnp.arange(pair_rows, dtype=jnp.int32)
    head_of = rows // resident
    slot_of = rows % resident
    match = slots[None, :] == slot_of[:, None]
    sequence = jnp.sum(jnp.where(match, jnp.arange(resident, dtype=jnp.int32)[None, :], 0), axis=1)
    grouped = queries.reshape(resident, heads, group, width)
    query_rows = grouped[sequence, head_of]
    own = new_kv[sequence, head_of]
    own_key = own[:, 0]
    own_value = own[:, 1].astype(jnp.float32)
    live_len = lengths[sequence]
    scores = (
        jnp.einsum("rgd,rpd->rgp", query_rows, k_cache, preferred_element_type=jnp.float32)
        * query_scale
    )
    own_score = (
        jnp.einsum("rgd,rd->rg", query_rows, own_key, preferred_element_type=jnp.float32)
        * query_scale
    )
    cache_pos = lax.axis_index("tp") * span + jnp.arange(span, dtype=jnp.int32)
    live = cache_pos[None, None, :] < live_len[:, None, None]
    masked = jnp.where(live, scores, negative)
    local_top = jnp.max(masked, axis=2)
    weights = jnp.where(live, jnp.exp(masked - local_top[..., None]), 0.0)
    partial_value = jnp.einsum(
        "rgp,rpd->rgd", weights.astype(jnp.bfloat16), v_cache, preferred_element_type=jnp.float32
    )
    upper, total, summed = merged(
        (local_top, jnp.sum(weights, axis=2), partial_value), "tp", combine_parts
    )
    overall = jnp.maximum(upper, own_score)
    rescale = jnp.exp(upper - overall)
    own_weight = jnp.exp(own_score - overall)
    total = total * rescale + own_weight
    summed = summed * rescale[..., None] + own_weight[..., None] * own_value[:, None, :]
    attended = (summed / total[..., None]).astype(jnp.bfloat16).reshape(pair_rows, group * width)
    return (prompt_owned, attended)


def solution(mesh):
    in_specs = (
        P(("groups", "seq", "tp"), None, None),
        P("groups"),
        P("groups", None),
        P("groups", None, None, None),
        P(("groups", "seq"), "tp", None),
        P(("groups", "seq"), "tp", None),
        P("groups"),
        P("groups"),
    )
    out_specs = (P(("groups", "tp"), "seq", None), P(("groups", "seq"), None))
    return jax.shard_map(
        per_device, mesh=mesh, in_specs=in_specs, out_specs=out_specs, check_vma=False
    )
```

profile of v0, /device:TPU:0, one launch (start us, length us, event | category | flops | bytes accessed | tf_op | source)
XLA Modules:
  0.0 412.0 jit_solution(3879226195800347556)
XLA Ops:
  1.3 20.4 %copy_select_fusion = bf16[1024,64,128]{2,0,1:T(8,128)(2,1)} fusion(bf16[1024,64,128]{2,1,0:T(8,128)(2,1)} %param.10, pred[1024]{0:T(1024)(128)(4,1)S(1)} %add_compare_fusion), kind=kLoop, calls=%fused_computation.12 | loop fusion | flops 8388608 | bytes 33555456 | tf_op jit(solution)/shard_map/jit(_where)/select_n | solution.py:34
  21.7 7.1 %all-to-all-start = ((bf16[1024,64,128]{2,0,1:T(8,128)(2,1)}), bf16[1024,64,128]{2,0,1:T(8,128)(2,1)}, u32[]{:S(2)}, u32[]{:S(2)}) async-start(bf16[1024,64,128]{2,0,1:T(8,128)(2,1)} %copy_select_fusion), calls=%async_computation | async-start | bytes 33554432 | tf_op jit(solution)/shard_map/all_to_all | solution.py:37
  29.1 0.7 gather_fusion.1
  29.7 0.7 gather_fusion
  30.4 0.1 broadcast_compare_fusion
  30.5 10.3 %fusion.21 = (f32[32,2]{1,0:T(8,128)S(1)}, f32[32,2,2048]{2,1,0:T(2,128)S(1)}) fusion(bf16[32,2,128]{2,1,0:T(2,128)(2,1)S(1)} %gather_fusion.1, bf16[32,2048,128]{2,1,0:T(8,128)(2,1)} %param.14, pred[32,2048]{1,0:T(8,128)(4,1)S(1)} %broadcast_compare_fusion), kind=kOutput, calls=%fused_computation.54 | convolution fusion | flops 33947584 | bytes 17383680 | tf_op jit(solution)/shard_map/rgd,rpd->rgp/dot_general | solution.py:56
  40.9 0.7 fusion.6
  41.7 7.1 %fusion.4 = f32[32,2,128]{2,1,0:T(2,128)S(1)} fusion(bf16[32,2048,128]{2,1,0:T(8,128)(2,1)} %param.15, f32[32,2,2048]{2,1,0:T(2,128)S(1)} %get-tuple-element.207, pred[32,2048]{1,0:T(8,128)(4,1)S(1)} %broadcast_compare_fusion, f32[32,2]{1,0:T(8,128)S(1)} %get-tuple-element.206), kind=kOutput, calls=%fused_computation.16 | convolution fusion | flops 33947648 | bytes 17400064 | tf_op jit(solution)/shard_map/rgp,rpd->rgd/dot_general | solution.py:68
  48.8 6.5 %all-gather.2 = f32[128,2,128]{2,1,0:T(2,128)S(1)} all-gather(f32[32,2,128]{2,1,0:T(2,128)S(1)} %fusion.4), channel_id=4, replica_groups=mesh['groups'=2,'seq'=4,'tp'=4] {'tp'}, dimensions={0}, use_global_device_ids=true | all-gather | bytes 163840 | tf_op jit(solution)/shard_map/all_gather | solution.py:11
  55.3 0.7 gather_fusion.2
  56.0 0.1 fusion.8
  56.2 5.2 %all-gather.3 = f32[4,32,2]{1,2,0:T(2,128)S(1)} all-gather(f32[1,32,2]{1,2,0:T(2,128)S(1)} %bitcast.67), channel_id=2, replica_groups=mesh['groups'=2,'seq'=4,'tp'=4] {'tp'}, dimensions={0}, use_global_device_ids=true | all-gather | bytes 1280 | tf_op jit(solution)/shard_map/all_gather | solution.py:11
  61.5 5.1 %all-gather.4 = f32[4,32,2]{1,2,0:T(2,128)S(1)} all-gather(f32[1,32,2]{1,2,0:T(2,128)S(1)} %bitcast.68), channel_id=3, replica_groups=mesh['groups'=2,'seq'=4,'tp'=4] {'tp'}, dimensions={0}, use_global_device_ids=true | all-gather | bytes 1280 | tf_op jit(solution)/shard_map/all_gather | solution.py:11
  66.5 1.3 while.19
  66.5 0.1 copy.57
  66.7 0.2 fusion.29
  67.2 0.2 fusion.29
  67.5 0.1 copy.58
  67.6 0.2 fusion.29
  67.9 0.1 copy.48
  68.2 0.2 fusion.7
  68.3 0.6 copy.54
  69.0 324.5 %all-to-all-done = bf16[1024,64,128]{2,0,1:T(8,128)(2,1)} async-done(((bf16[1024,64,128]{2,0,1:T(8,128)(2,1)}), bf16[1024,64,128]{2,0,1:T(8,128)(2,1)}, u32[]{:S(2)}, u32[]{:S(2)}) %all-to-all-start) | async-done | bytes 16777248 | tf_op jit(solution)/shard_map/all_to_all | solution.py:37
  393.4 18.6 %copy.43 = bf16[4,1024,16,128]{3,2,1,0:T(8,128)(2,1)} copy(bf16[4,1024,16,128]{3,1,2,0:T(8,128)(2,1)} %bitcast.5) | data formatting | bytes 33554432 | tf_op jit(solution)/shard_map/all_to_all | solution.py:37
  (32 shorter events, 1.1 us)
Async XLA Ops:
  0.6 54.7 %copy-start = (bf16[8,16,2,128]{3,2,1,0:T(2,128)(2,1)S(1)}, bf16[8,16,2,128]{3,2,1,0:T(2,128)(2,1)}, u32[]{:S(2)}) copy-start(bf16[8,16,2,128]{3,2,1,0:T(2,128)(2,1)} %param.13) | copy-start | bytes 196612
  21.7 7.1 %copy-start.2 = (bf16[8,4096]{1,0:T(8,128)(2,1)S(1)}, bf16[8,4096]{1,0:T(8,128)(2,1)}, u32[]{:S(2)}) copy-start(bf16[8,4096]{1,0:T(8,128)(2,1)} %param.12) | copy-start | bytes 196612
  21.7 7.2 %copy-start.3 = (s32[8]{0:T(128)S(1)}, s32[8]{0:T(128)}, u32[]{:S(2)}) copy-start(s32[8]{0:T(128)} %param.17) | copy-start | bytes 100
  21.7 8.0 %copy-start.1 = (s32[8]{0:T(128)S(1)}, s32[8]{0:T(128)}, u32[]{:S(2)}) copy-start(s32[8]{0:T(128)} %param.16) | copy-start | bytes 100
  21.7 371.7 %all-to-all-start = ((bf16[1024,64,128]{2,0,1:T(8,128)(2,1)}), bf16[1024,64,128]{2,0,1:T(8,128)(2,1)}, u32[]{:S(2)}, u32[]{:S(2)}) async-start(bf16[1024,64,128]{2,0,1:T(8,128)(2,1)} %copy_select_fusion), calls=%async_computation | async-start | bytes 33554432 | tf_op jit(solution)/shard_map/all_to_all | solution.py:37
where the time goes:
time: 413 us; the launch traced here: 412 us
  waiting for transfers between devices  324 us (78%)
  local copies, waits for them, and re-layouts  22.3 us (5%)
  other arithmetic  22.3 us (5%)
  matrix products  17.5 us (4%)
  blocking collectives  16.8 us (4%)
  starting transfers between devices  7.11 us (2%)
    all_to_all x1, waiting for transfers between devices, per_device(): lax.all_to_all(kept, 'seq', split_axis=1, concat_axis=0, tiled=True)  324 us
    select_n x1, other arithmetic, per_device(): jnp.where((position < prompt_length[0])[:, None, None], prompt_kv, jnp.ze...  20.4 us
    all_to_all x1, local copies, waits for them, and re-layouts, per_device(): lax.all_to_all(kept, 'seq', split_axis=1, concat_axis=0, tiled=True)  18.6 us
    all_gather x3, blocking collectives, merged(): gathered = jax.tree.map(lambda a: lax.all_gather(a, axis), part)  16.8 us
    dot_general x1, matrix products, per_device(): jnp.einsum('rgd,rpd->rgp', query_rows, k_cache, preferred_element_type=jn...  10.3 us
  transfers between devices with their start and end apart: 1, of which 1 were waited for; matrix products, arithmetic and copies ran while one was open for 6% of the time, Pallas kernels for 0%

commit v1 on v0

--- a/solution.py
+++ b/solution.py
@@ -34,7 +34,26 @@
     kept = jnp.where(
         (position < prompt_length[0])[:, None, None], prompt_kv, jnp.zeros_like(prompt_kv)
     )
-    prompt_owned = lax.all_to_all(kept, "seq", split_axis=1, concat_axis=0, tiled=True)
+
+    def pass_scenes(array_in, dim_no, dim_k):
+        axis_tag = "seq"
+        after = jax.lax.axis_index(axis_tag)
+        response = jax.lax.axis_size(axis_tag)
+        row_out, local_now = (response, after)
+        x_new = array_in.shape[dim_k] // row_out
+        value_now = jnp.roll(array_in, -local_now * x_new, dim_k)
+        z2 = lax.slice_in_dim(value_now, 0, x_new, axis=dim_k)
+        crops = [z2]
+        for b in range(1, row_out):
+            k_now = lax.slice_in_dim(value_now, b * x_new, (b + 1) * x_new, axis=dim_k)
+            answer = jax.lax.ppermute(
+                k_now, axis_tag, [(t, (t + b) % row_out) for t in range(row_out)]
+            )
+            crops.append(answer)
+        s_next = jnp.concatenate(crops[::-1], dim_no)
+        return jnp.roll(s_next, (local_now + 1) * crops[0].shape[dim_no], axis=dim_no)
+
+    prompt_owned = pass_scenes(kept, 0, 1)
     resident = lengths.shape[0]
     pair_rows = k_cache.shape[0]
     span = k_cache.shape[1]

time: 413 us -> 454 us (1.099)
  local copies, waits for them, and re-layouts: 22.3 us -> 68.8 us
  waiting for transfers between devices: 324 us -> 315 us
  other arithmetic: 22.3 us -> 28.8 us
    all_to_all x1 -> x0, waiting for transfers between devices: 324 us -> none  [per_device(): lax.all_to_all(kept, 'seq', split_axis=1, concat_axis=0, tiled=True)]
    ppermute x0 -> x3, waiting for transfers between devices: none -> 315 us  [pass_scenes(): jax.lax.ppermute(k_now, axis_tag, [(t, (t + b) % row_out) for t in range(...]
    unnamed x9 -> x18, local copies, waits for them, and re-layouts: 0.63 us -> 40.8 us
    all_to_all x1 -> x0, local copies, waits for them, and re-layouts: 18.6 us -> none  [per_device(): lax.all_to_all(kept, 'seq', split_axis=1, concat_axis=0, tiled=True)]
    dynamic_slice x0 -> x1, local copies, waits for them, and re-layouts: none -> 14.5 us  [pass_scenes(): jnp.roll(s_next, (local_now + 1) * crops[0].shape[dim_no], axis=dim_no)]
    concatenate x0 -> x1, other arithmetic: none -> 11.8 us  [pass_scenes(): value_now = jnp.roll(array_in, -local_now * x_new, dim_k)]
    all_to_all x1 -> x0, starting transfers between devices: 7.11 us -> none  [per_device(): lax.all_to_all(kept, 'seq', split_axis=1, concat_axis=0, tiled=True)]
    ppermute x0 -> x3, starting transfers between devices: none -> 5.94 us  [pass_scenes(): jax.lax.ppermute(k_now, axis_tag, [(t, (t + b) % row_out) for t in range(...]
  transfers between devices with their start and end apart: 1 -> 3, of which waited for: 1 -> 2; matrix products, arithmetic and copies ran while one was open for 6% -> 7% of each run, Pallas kernels for 0% -> 0%
where the time goes in v1:
time: 454 us; the launch traced here: 453 us
  waiting for transfers between devices  315 us (69%)
  local copies, waits for them, and re-layouts  68.8 us (15%)
  other arithmetic  28.8 us (6%)
  matrix products  17.5 us (4%)
  blocking collectives  15.7 us (3%)
  starting transfers between devices  5.94 us (1%)
    ppermute x3, waiting for transfers between devices, pass_scenes(): jax.lax.ppermute(k_now, axis_tag, [(t, (t + b) % row_out) for t in range(...  315 us
    unnamed x18, local copies, waits for them, and re-layouts  40.8 us
    all_gather x3, blocking collectives, merged(): gathered = jax.tree.map(lambda a: lax.all_gather(a, axis), part)  15.7 us
    select_n x1, other arithmetic, per_device(): jnp.where((position < prompt_length[0])[:, None, None], prompt_kv, jnp.ze...  15 us
    dynamic_slice x1, local copies, waits for them, and re-layouts, pass_scenes(): jnp.roll(s_next, (local_now + 1) * crops[0].shape[dim_no], axis=dim_no)  14.5 us
    concatenate x1, other arithmetic, pass_scenes(): value_now = jnp.roll(array_in, -local_now * x_new, dim_k)  11.8 us
    dot_general x1, matrix products, per_device(): jnp.einsum('rgd,rpd->rgp', query_rows, k_cache, preferred_element_type=jn...  10.3 us
  transfers between devices with their start and end apart: 3, of which 2 were waited for; matrix products, arithmetic and copies ran while one was open for 7% of the time, Pallas kernels for 0%

profile of v1, /device:TPU:0, one launch (start us, length us, event | category | flops | bytes accessed | tf_op | source)
XLA Modules:
  0.0 453.0 jit_solution(11773508913194874765)
XLA Ops:
  1.4 15.0 %broadcast_select_fusion = bf16[1024,64,128]{2,1,0:T(8,128)(2,1)} fusion(bf16[1024,64,128]{2,1,0:T(8,128)(2,1)} %param.10, pred[1024]{0:T(1024)(128)(4,1)S(1)} %add_compare_fusion), kind=kLoop, calls=%fused_computation.15 | loop fusion | flops 8388608 | bytes 33555456 | tf_op jit(solution)/shard_map/jit(_where)/select_n | solution.py:34
  16.4 11.8 %fusion.3 = bf16[1024,64,128]{2,1,0:T(8,128)(2,1)S(1)} fusion(s32[]{:T(128)S(6)} %select_n.102, bf16[1024,64,128]{2,1,0:T(8,128)(2,1)} %broadcast_select_fusion), kind=kLoop, calls=%fused_computation.14 | loop fusion | flops 33554432 | bytes 33554436 | tf_op jit(solution)/shard_map/jit(_roll_dynamic)/concatenate | solution.py:44
  28.2 6.2 %copy-done.2 = bf16[1024,64,128]{2,1,0:T(8,128)(2,1)} copy-done((bf16[1024,64,128]{2,1,0:T(8,128)(2,1)}, bf16[1024,64,128]{2,1,0:T(8,128)(2,1)S(1)}, u32[]{:S(2)}) %copy-start.2) | copy-done | bytes 16777240
  34.4 5.5 %fusion.22 = (bf16[1024,16,128]{2,1,0:T(8,128)(2,1)}, bf16[1024,16,128]{2,1,0:T(8,128)(2,1)}, bf16[1024,16,128]{2,1,0:T(8,128)(2,1)}) fusion(bf16[1024,64,128]{2,1,0:T(8,128)(2,1)S(1)} %fusion.3), kind=kLoop, calls=%fused_computation.66 | loop fusion | bytes 25165824 | tf_op jit(solution)/shard_map/slice | solution.py:48
  39.9 5.0 %collective-permute-start = (bf16[1024,16,128]{2,1,0:T(8,128)(2,1)}, bf16[1024,16,128]{2,1,0:T(8,128)(2,1)}, u32[]{:S(2)}, u32[]{:S(2)}) collective-permute-start(bf16[1024,16,128]{2,1,0:T(8,128)(2,1)} %get-tuple-element.206), channel_id=1, source_target_pairs={{0,12},{4,0},{8,4},{12,8},{1,13},{5,1},{9,5},{13,9},{2,14},{6,2},{... | collective-permute-start | bytes 12582920 | tf_op jit(solution)/shard_map/ppermute | solution.py:49
  44.8 1.0 collective-permute-start.2
  47.5 10.3 %fusion.23 = (f32[32,2]{1,0:T(8,128)S(1)}, f32[32,2,2048]{2,1,0:T(2,128)S(1)}) fusion(bf16[32,2,128]{2,1,0:T(2,128)(2,1)S(1)} %gather_fusion.1, bf16[32,2048,128]{2,1,0:T(8,128)(2,1)} %param.14, pred[32,2048]{1,0:T(8,128)(4,1)S(1)} %broadcast_compare_fusion), kind=kOutput, calls=%fused_computation.67 | convolution fusion | flops 33947584 | bytes 17383680 | tf_op jit(solution)/shard_map/rgd,rpd->rgp/dot_general | solution.py:75
  57.9 7.1 %fusion.5 = f32[32,2,128]{2,1,0:T(2,128)S(1)} fusion(bf16[32,2048,128]{2,1,0:T(8,128)(2,1)} %param.15, f32[32,2,2048]{2,1,0:T(2,128)S(1)} %get-tuple-element.210, pred[32,2048]{1,0:T(8,128)(4,1)S(1)} %broadcast_compare_fusion, f32[32,2]{1,0:T(8,128)S(1)} %get-tuple-element.209), kind=kOutput, calls=%fused_computation.21 | convolution fusion | flops 33947648 | bytes 17400064 | tf_op jit(solution)/shard_map/rgp,rpd->rgd/dot_general | solution.py:87
  65.0 5.4 %all-gather.2 = f32[128,2,128]{2,1,0:T(2,128)S(1)} all-gather(f32[32,2,128]{2,1,0:T(2,128)S(1)} %fusion.5), channel_id=4, replica_groups=mesh['groups'=2,'seq'=4,'tp'=4] {'tp'}, dimensions={0}, use_global_device_ids=true | all-gather | bytes 163840 | tf_op jit(solution)/shard_map/all_gather | solution.py:11
  70.4 0.7 fusion.7
  72.1 5.1 %all-gather.4 = f32[4,32,2]{1,2,0:T(2,128)S(1)} all-gather(f32[1,32,2]{1,2,0:T(2,128)S(1)} %bitcast.63), channel_id=3, replica_groups=mesh['groups'=2,'seq'=4,'tp'=4] {'tp'}, dimensions={0}, use_global_device_ids=true | all-gather | bytes 1280 | tf_op jit(solution)/shard_map/all_gather | solution.py:11
  77.1 5.2 %all-gather.3 = f32[4,32,2]{1,2,0:T(2,128)S(1)} all-gather(f32[1,32,2]{1,2,0:T(2,128)S(1)} %bitcast.62), channel_id=2, replica_groups=mesh['groups'=2,'seq'=4,'tp'=4] {'tp'}, dimensions={0}, use_global_device_ids=true | all-gather | bytes 1280 | tf_op jit(solution)/shard_map/all_gather | solution.py:11
  82.4 1.3 while.19
  84.8 51.4 %collective-permute-done = bf16[1024,16,128]{2,1,0:T(8,128)(2,1)} collective-permute-done((bf16[1024,16,128]{2,1,0:T(8,128)(2,1)}, bf16[1024,16,128]{2,1,0:T(8,128)(2,1)}, u32[]{:S(2)}, u32[]{:S(2)}) %collective-permute-start) | collective-permute-done | bytes 4194336 | tf_op jit(solution)/shard_map/ppermute | solution.py:49
  136.2 4.8 %constant_dynamic-update-slice_fusion.5 = bf16[8192,16,128]{2,1,0:T(8,128)(2,1)} fusion(bf16[1024,16,128]{2,1,0:T(8,128)(2,1)} %collective-permute-done), kind=kLoop, calls=%fused_computation.35 | loop fusion | bytes 8388608
  141.0 263.4 %collective-permute-done.1 = bf16[1024,16,128]{2,1,0:T(8,128)(2,1)} collective-permute-done((bf16[1024,16,128]{2,1,0:T(8,128)(2,1)}, bf16[1024,16,128]{2,1,0:T(8,128)(2,1)}, u32[]{:S(2)}, u32[]{:S(2)}) %collective-permute-start.1) | collective-permute-done | bytes 4194336 | tf_op jit(solution)/shard_map/ppermute | solution.py:49
  404.4 4.9 %constant_dynamic-update-slice_fusion.4 = bf16[8192,16,128]{2,1,0:T(8,128)(2,1)} fusion(bf16[8192,16,128]{2,1,0:T(8,128)(2,1)} %constant_dynamic-update-slice_fusion.5, bf16[1024,16,128]{2,1,0:T(8,128)(2,1)} %collective-permute-done.1), kind=kLoop, calls=%fused_computation.34 | loop fusion | bytes 8388608
  409.3 4.9 %constant_dynamic-update-slice_fusion.3 = bf16[8192,16,128]{2,1,0:T(8,128)(2,1)} fusion(bf16[8192,16,128]{2,1,0:T(8,128)(2,1)} %constant_dynamic-update-slice_fusion.4, bf16[1024,16,128]{2,1,0:T(8,128)(2,1)} %collective-permute-done.2), kind=kLoop, calls=%fused_computation.33 | loop fusion | bytes 8388608
  414.1 4.9 %slice_dynamic-update-slice_fusion = bf16[8192,16,128]{2,1,0:T(8,128)(2,1)} fusion(bf16[8192,16,128]{2,1,0:T(8,128)(2,1)} %constant_dynamic-update-slice_fusion.3, bf16[1024,64,128]{2,1,0:T(8,128)(2,1)} %copy-done.2), kind=kLoop, calls=%fused_computation.16 | loop fusion | bytes 8388608
  419.0 4.8 %constant_dynamic-update-slice_fusion.2 = bf16[8192,16,128]{2,1,0:T(8,128)(2,1)} fusion(bf16[8192,16,128]{2,1,0:T(8,128)(2,1)} %slice_dynamic-update-slice_fusion, bf16[1024,16,128]{2,1,0:T(8,128)(2,1)} %collective-permute-done), kind=kLoop, calls=%fused_computation.32 | loop fusion | bytes 8388608
  423.8 4.9 %constant_dynamic-update-slice_fusion.1 = bf16[8192,16,128]{2,1,0:T(8,128)(2,1)} fusion(bf16[8192,16,128]{2,1,0:T(8,128)(2,1)} %constant_dynamic-update-slice_fusion.2, bf16[1024,16,128]{2,1,0:T(8,128)(2,1)} %collective-permute-done.1), kind=kLoop, calls=%fused_computation.31 | loop fusion | bytes 8388608
  428.7 4.9 %constant_dynamic-update-slice_fusion = bf16[8192,16,128]{2,1,0:T(8,128)(2,1)} fusion(bf16[8192,16,128]{2,1,0:T(8,128)(2,1)} %constant_dynamic-update-slice_fusion.1, bf16[1024,16,128]{2,1,0:T(8,128)(2,1)} %collective-permute-done.2), kind=kLoop, calls=%fused_computation.30 | loop fusion | bytes 8388608
  433.6 4.9 %slice_dynamic-update-slice_fusion.1 = bf16[8192,16,128]{2,1,0:T(8,128)(2,1)} fusion(bf16[8192,16,128]{2,1,0:T(8,128)(2,1)} %constant_dynamic-update-slice_fusion, bf16[1024,64,128]{2,1,0:T(8,128)(2,1)} %copy-done.2), kind=kLoop, calls=%fused_computation.17 | loop fusion | bytes 8388608 | tf_op jit(solution)/shard_map/jit(_roll_dynamic)/concatenate | solution.py:54
  438.5 14.5 %constant_dynamic-slice_fusion.1 = bf16[4096,16,128]{2,1,0:T(8,128)(2,1)} fusion(bf16[8192,16,128]{2,1,0:T(8,128)(2,1)} %slice_dynamic-update-slice_fusion.1, s32[]{:T(128)S(6)} %select_n.104), kind=kLoop, calls=%fused_computation.58 | loop fusion | bytes 33554436 | tf_op jit(solution)/shard_map/jit(_roll_dynamic)/dynamic_slice | solution.py:54
  (48 shorter events, 5.1 us)
Async XLA Ops:
  0.6 70.5 %copy-start = (bf16[8,16,2,128]{3,2,1,0:T(2,128)(2,1)S(1)}, bf16[8,16,2,128]{3,2,1,0:T(2,128)(2,1)}, u32[]{:S(2)}) copy-start(bf16[8,16,2,128]{3,2,1,0:T(2,128)(2,1)} %param.13) | copy-start | bytes 196612
  28.2 6.2 %copy-start.2 = (bf16[1024,64,128]{2,1,0:T(8,128)(2,1)}, bf16[1024,64,128]{2,1,0:T(8,128)(2,1)S(1)}, u32[]{:S(2)}) copy-start(bf16[1024,64,128]{2,1,0:T(8,128)(2,1)S(1)} %fusion.3) | copy-start | bytes 50331652
  34.4 11.4 %copy-start.4 = (s32[8]{0:T(128)S(1)}, s32[8]{0:T(128)}, u32[]{:S(2)}) copy-start(s32[8]{0:T(128)} %param.17) | copy-start | bytes 100
  34.4 11.6 %copy-start.3 = (bf16[8,4096]{1,0:T(8,128)(2,1)S(1)}, bf16[8,4096]{1,0:T(8,128)(2,1)}, u32[]{:S(2)}) copy-start(bf16[8,4096]{1,0:T(8,128)(2,1)} %param.12) | copy-start | bytes 196612
  34.4 11.6 %copy-start.1 = (s32[8]{0:T(128)S(1)}, s32[8]{0:T(128)}, u32[]{:S(2)}) copy-start(s32[8]{0:T(128)} %param.16) | copy-start | bytes 100
  39.9 96.3 %collective-permute-start = (bf16[1024,16,128]{2,1,0:T(8,128)(2,1)}, bf16[1024,16,128]{2,1,0:T(8,128)(2,1)}, u32[]{:S(2)}, u32[]{:S(2)}) collective-permute-start(bf16[1024,16,128]{2,1,0:T(8,128)(2,1)} %get-tuple-element.206), channel_id=1, source_target_pairs={{0,12},{4,0},{8,4},{12,8},{1,13},{5,1},{9,5},{13,9},{2,14},{6,2},{... | collective-permute-start | bytes 12582920 | tf_op jit(solution)/shard_map/ppermute | solution.py:49
  44.8 359.5 %collective-permute-start.1 = (bf16[1024,16,128]{2,1,0:T(8,128)(2,1)}, bf16[1024,16,128]{2,1,0:T(8,128)(2,1)}, u32[]{:S(2)}, u32[]{:S(2)}) collective-permute-start(bf16[1024,16,128]{2,1,0:T(8,128)(2,1)} %get-tuple-element.205), channel_id=1, source_target_pairs={{0,8},{4,12},{8,0},{12,4},{1,9},{5,13},{9,1},{13,5},{2,10},{6,14},... | collective-permute-start | bytes 12582920 | tf_op jit(solution)/shard_map/ppermute | solution.py:49
  44.8 364.4 %collective-permute-start.2 = (bf16[1024,16,128]{2,1,0:T(8,128)(2,1)}, bf16[1024,16,128]{2,1,0:T(8,128)(2,1)}, u32[]{:S(2)}, u32[]{:S(2)}) collective-permute-start(bf16[1024,16,128]{2,1,0:T(8,128)(2,1)} %get-tuple-element.204), channel_id=1, source_target_pairs={{0,4},{4,8},{8,12},{12,0},{1,5},{5,9},{9,13},{13,1},{2,6},{6,10},{... | collective-permute-start | bytes 12582920 | tf_op jit(solution)/shard_map/ppermute | solution.py:49
